TPU v7x, 32 devices: a whole 2x2x4 slice. The times are simulated.
32 devices in a mesh: dp: 2 (over y), seq: 16 (over z, x, core).
Axes of the slice: x: 2, y: 2, z: 4, core: 2. Of those that a mesh axis runs over, the one named last changes fastest.
Arguments:
- tokens: bfloat16 [2, 8192, 1024], P('dp', 'seq'), may hold values from -18 to 18
- lengths: int32 [2, 64], P('dp'), may hold values from 1 to 128
- w_query: bfloat16 [1024, 512], replicated, may hold values from -0.1875 to 0.1875
- w_key: bfloat16 [1024, 512], replicated, may hold values from -0.1875 to 0.1875
- w_value: bfloat16 [1024, 512], replicated, may hold values from -0.1875 to 0.1875
- w_out: bfloat16 [512, 1024], replicated, may hold values from -2 to 2
- cotangent: bfloat16 [2, 8192, 1024], P('dp', 'seq'), may hold values from -6 to 6
Outputs:
- mixed: bfloat16 [2, 8192, 1024], P('dp', 'seq')
- grad_tokens: bfloat16 [2, 8192, 1024], P('dp', 'seq')
- grad_query: float32 [1024, 512], replicated
- grad_key: float32 [1024, 512], replicated
- grad_value: float32 [1024, 512], replicated
- grad_output: float32 [512, 1024], replicated
All inputs are finite; a program needn't handle non-finite values.
Results may differ from a plain program's by a relative error of at most 0.014.
The roundings to bfloat16 on the way count: a program that leaves them out, or rounds other values in their place, can miss the bound.
Values may be sent and summed in bfloat16 or wider, within the bound.
No kernel may reach another device: no remote copies, remote signals or barrier semaphores. Data moves between devices by JAX's collectives and lax.ppermute only.
A program may use at most 192 MiB of HBM per device.

v0:
```python
import math
import jax
import jax.numpy as jnp
from jax import lax
from jax.sharding import PartitionSpec as P

HEADS = 4
TILE = 128
bar_offsets = (0, 1, 2, 4, 8, 12, 16, 24, 32)
group_bars = 4
far_score = -1e30


def shifted(block, axis, distance):
    devices = range(lax.axis_size(axis))
    route = [(i - distance, i) for i in devices if i - distance in devices]
    return lax.ppermute(block, axis, route)


def product(form, left, right):
    return jnp.einsum(form, left, right, preferred_element_type=jnp.float32)


def summarize(bar_rows, length):
    slot_ids = jnp.arange(bar_rows.shape[1], dtype=jnp.int32)
    live_slots = slot_ids[None, :] < length[:, None]
    running = jnp.sum(jnp.where(live_slots[:, :, None], bar_rows.astype(jnp.float32), 0.0), axis=1)
    return (running / length[:, None].astype(jnp.float32)).astype(jnp.bfloat16)


def bar_block(
    queries,
    ext_key,
    ext_value,
    ext_length,
    base_bar,
    bar_ids,
    query_length,
    summary_key,
    summary_value,
    grad_context,
):
    group_count, tile_len, head_count, head_dim = queries.shape
    sources = len(bar_offsets)
    key_parts = []
    value_parts = []
    length_parts = []
    for offset in bar_offsets:
        first_bar = base_bar - offset
        key_parts.append(lax.dynamic_slice_in_dim(ext_key, first_bar, group_count, 0))
        value_parts.append(lax.dynamic_slice_in_dim(ext_value, first_bar, group_count, 0))
        length_parts.append(lax.dynamic_slice_in_dim(ext_length, first_bar, group_count, 0))
    fine_key = jnp.stack(key_parts, 1).reshape(
        group_count, sources * tile_len, head_count, head_dim
    )
    fine_value = jnp.stack(value_parts, 1).reshape(
        group_count, sources * tile_len, head_count, head_dim
    )
    fine_length = jnp.stack(length_parts, 1)
    slot_ids = jnp.arange(tile_len, dtype=jnp.int32)
    key_live = slot_ids[None, None, :] < fine_length[:, :, None]
    causal = slot_ids[None, :] <= slot_ids[:, None]
    other_bar = jnp.arange(sources, dtype=jnp.int32) != 0
    fine_live = key_live[:, None, :, :] & (
        causal[None, :, None, :] | other_bar[None, None, :, None]
    )
    fine_live = fine_live.reshape(group_count, 1, tile_len, sources * tile_len)
    distance = bar_ids[:, None] - jnp.arange(summary_key.shape[0], dtype=jnp.int32)[None, :]
    coarse_live = distance >= 1
    for offset in bar_offsets[1:]:
        coarse_live = coarse_live & (distance != offset)
    coarse_live = coarse_live[:, None, None, :]
    score_scale = 1.0 / math.sqrt(head_dim)
    fine_score = product("gqhe,gkhe->ghqk", queries, fine_key) * score_scale
    coarse_score = product("gqhe,nhe->ghqn", queries, summary_key) * score_scale
    fine_score = jnp.where(fine_live, fine_score, far_score)
    coarse_score = jnp.where(coarse_live, coarse_score, far_score)
    top_score = jnp.maximum(jnp.max(fine_score, axis=-1), jnp.max(coarse_score, axis=-1))[..., None]
    fine_exp = jnp.where(fine_live, jnp.exp(fine_score - top_score), 0.0)
    coarse_exp = jnp.where(coarse_live, jnp.exp(coarse_score - top_score), 0.0)
    denominator = (jnp.sum(fine_exp, axis=-1) + jnp.sum(coarse_exp, axis=-1))[..., None]
    fine_prob = fine_exp / denominator
    coarse_prob = coarse_exp / denominator
    fine_round = fine_prob.astype(jnp.bfloat16)
    coarse_round = coarse_prob.astype(jnp.bfloat16)
    attended_context = product("ghqk,gkhe->gqhe", fine_round, fine_value) + product(
        "ghqn,nhe->gqhe", coarse_round, summary_value
    )
    query_live = slot_ids[None, :] < query_length[:, None]
    attended_context = jnp.where(query_live[:, :, None, None], attended_context, 0.0)
    fine_dp = product("gqhe,gkhe->ghqk", grad_context, fine_value)
    coarse_dp = product("gqhe,nhe->ghqn", grad_context, summary_value)
    delta = (jnp.sum(fine_prob * fine_dp, axis=-1) + jnp.sum(coarse_prob * coarse_dp, axis=-1))[
        ..., None
    ]
    fine_ds = (fine_prob * (fine_dp - delta) * score_scale).astype(jnp.bfloat16)
    coarse_ds = (coarse_prob * (coarse_dp - delta) * score_scale).astype(jnp.bfloat16)
    query_gradient_rows = product("ghqk,gkhe->gqhe", fine_ds, fine_key) + product(
        "ghqn,nhe->gqhe", coarse_ds, summary_key
    )
    fine_gk = product("ghqk,gqhe->gkhe", fine_ds, queries).reshape(
        group_count, sources, tile_len, head_count, head_dim
    )
    fine_gv = product("ghqk,gqhe->gkhe", fine_round, grad_context).reshape(
        group_count, sources, tile_len, head_count, head_dim
    )
    coarse_key_gradient = product("ghqn,gqhe->nhe", coarse_ds, queries)
    coarse_value_gradient = product("ghqn,gqhe->nhe", coarse_round, grad_context)
    return (
        attended_context,
        query_gradient_rows,
        fine_gk,
        fine_gv,
        coarse_key_gradient,
        coarse_value_gradient,
    )


def spread(running, grads, base_bar):
    group_count = grads.shape[0]
    for position, offset in enumerate(bar_offsets):
        first_bar = base_bar - offset
        current = lax.dynamic_slice_in_dim(running, first_bar, group_count, 0)
        running = lax.dynamic_update_slice_in_dim(
            running, current + grads[:, position], first_bar, 0
        )
    return running


def local(tokens, lengths, w_query, w_key, w_value, w_out, cotangent):
    inputs = tokens[0]
    grad_out = cotangent[0]
    token_count = inputs.shape[0]
    inner_width = w_query.shape[1]
    head_dim = inner_width // HEADS
    bar_count = token_count // TILE
    reach_dev = max(bar_offsets[-1] // bar_count, 1)
    queries = jnp.dot(inputs, w_query, preferred_element_type=jnp.float32).astype(jnp.bfloat16)
    keys_own = jnp.dot(inputs, w_key, preferred_element_type=jnp.float32).astype(jnp.bfloat16)
    values_own = jnp.dot(inputs, w_value, preferred_element_type=jnp.float32).astype(jnp.bfloat16)
    all_length = lengths[0]
    first_own = lax.axis_index("seq") * bar_count
    local_length = lax.dynamic_slice_in_dim(all_length, first_own, bar_count, 0)
    slot_ids = jnp.arange(TILE, dtype=jnp.int32)
    live_slots = slot_ids[None, :] < local_length[:, None]
    token_live = live_slots.reshape(-1)
    own_summary = (
        summarize(keys_own.reshape(bar_count, TILE, inner_width), local_length),
        summarize(values_own.reshape(bar_count, TILE, inner_width), local_length),
    )
    summary_key, summary_value = (
        lax.all_gather(own_summary[0], "seq", axis=0, tiled=True),
        lax.all_gather(own_summary[1], "seq", axis=0, tiled=True),
    )
    summary_key = summary_key.reshape(-1, HEADS, head_dim)
    summary_value = summary_value.reshape(-1, HEADS, head_dim)
    grad_context = jnp.dot(grad_out, w_out.T, preferred_element_type=jnp.float32)
    grad_context = jnp.where(token_live[:, None], grad_context, 0.0).astype(jnp.bfloat16)
    key_stack = keys_own[None]
    value_stack = values_own[None]
    for level_bit in range(reach_dev.bit_length() - 1):
        arrived = shifted((key_stack, value_stack), "seq", 1 << level_bit)
        key_stack = jnp.concatenate([key_stack, arrived[0]], 0)
        value_stack = jnp.concatenate([value_stack, arrived[1]], 0)
    arrived = shifted((key_stack[:1], value_stack[:1]), "seq", reach_dev)
    key_stack = jnp.concatenate([key_stack, arrived[0]], 0)
    value_stack = jnp.concatenate([value_stack, arrived[1]], 0)
    ext_bars = (reach_dev + 1) * bar_count
    ext_key = key_stack[::-1].reshape(ext_bars, TILE, HEADS, head_dim)
    ext_value = value_stack[::-1].reshape(ext_bars, TILE, HEADS, head_dim)
    padded_length = jnp.concatenate([jnp.zeros((reach_dev * bar_count,), jnp.int32), all_length], 0)
    ext_length = lax.dynamic_slice_in_dim(padded_length, first_own, ext_bars, 0)
    query_bars = queries.reshape(bar_count, TILE, HEADS, head_dim)
    grad_bars = grad_context.reshape(bar_count, TILE, HEADS, head_dim)

    def step(carried_state, block_index):
        accumulated_key, accumulated_value, accumulated_summary_key, accumulated_summary_value = (
            carried_state
        )
        begin_bar = block_index * group_bars
        base_bar = reach_dev * bar_count + begin_bar
        bar_ids = first_own + begin_bar + jnp.arange(group_bars, dtype=jnp.int32)
        result = bar_block(
            query_bars,
            ext_key,
            ext_value,
            ext_length,
            base_bar,
            bar_ids,
            local_length,
            summary_key,
            summary_value,
            grad_bars,
        )
        (
            attended_context,
            query_gradient_rows,
            fine_gk,
            fine_gv,
            coarse_key_gradient,
            coarse_value_gradient,
        ) = result
        accumulated_key = spread(accumulated_key, fine_gk, base_bar)
        accumulated_value = spread(accumulated_value, fine_gv, base_bar)
        return (
            (
                accumulated_key,
                accumulated_value,
                accumulated_summary_key + coarse_key_gradient,
                accumulated_summary_value + coarse_value_gradient,
            ),
            (attended_context.astype(jnp.bfloat16), query_gradient_rows.astype(jnp.bfloat16)),
        )

    ext_zero = jnp.zeros((ext_bars, TILE, HEADS, head_dim), jnp.float32)
    sum_zero = jnp.zeros(summary_key.shape, jnp.float32)
    carried_state, stacked = lax.scan(
        step,
        (ext_zero, ext_zero, sum_zero, sum_zero),
        jnp.arange(bar_count // group_bars, dtype=jnp.int32),
    )
    accumulated_key, accumulated_value, accumulated_summary_key, accumulated_summary_value = (
        carried_state
    )
    attended_context = stacked[0].reshape(token_count, inner_width)
    query_gradient_rows = stacked[1].reshape(token_count, inner_width)
    grad_key_stack = accumulated_key.reshape(reach_dev + 1, token_count, inner_width)[::-1]
    grad_value_stack = accumulated_value.reshape(reach_dev + 1, token_count, inner_width)[::-1]
    returned = (
        shifted(grad_key_stack[reach_dev:].astype(jnp.bfloat16), "seq", -reach_dev).astype(
            jnp.float32
        ),
        shifted(grad_value_stack[reach_dev:].astype(jnp.bfloat16), "seq", -reach_dev).astype(
            jnp.float32
        ),
    )
    grad_key_stack = grad_key_stack.at[0:1].add(returned[0])
    grad_value_stack = grad_value_stack.at[0:1].add(returned[1])
    for level_bit in reversed(range(reach_dev.bit_length() - 1)):
        half_span = 1 << level_bit
        returned = (
            shifted(
                grad_key_stack[half_span : 2 * half_span].astype(jnp.bfloat16), "seq", -half_span
            ).astype(jnp.float32),
            shifted(
                grad_value_stack[half_span : 2 * half_span].astype(jnp.bfloat16), "seq", -half_span
            ).astype(jnp.float32),
        )
        grad_key_stack = grad_key_stack.at[:half_span].add(returned[0])
        grad_value_stack = grad_value_stack.at[:half_span].add(returned[1])
    own_key = grad_key_stack[0]
    own_value = grad_value_stack[0]
    summary_back = (
        lax.psum_scatter(
            accumulated_summary_key.astype(jnp.bfloat16), "seq", scatter_dimension=0, tiled=True
        ).astype(jnp.float32),
        lax.psum_scatter(
            accumulated_summary_value.astype(jnp.bfloat16), "seq", scatter_dimension=0, tiled=True
        ).astype(jnp.float32),
    )
    inverse_denominator = 1.0 / local_length.astype(jnp.float32)
    shared_key_rows = summary_back[0].reshape(bar_count, inner_width) * inverse_denominator[:, None]
    share_value = summary_back[1].reshape(bar_count, inner_width) * inverse_denominator[:, None]
    own_key = own_key.reshape(bar_count, TILE, inner_width) + jnp.where(
        live_slots[:, :, None], shared_key_rows[:, None, :], 0.0
    )
    own_value = own_value.reshape(bar_count, TILE, inner_width) + jnp.where(
        live_slots[:, :, None], share_value[:, None, :], 0.0
    )
    grad_keys = own_key.reshape(token_count, inner_width).astype(jnp.bfloat16)
    grad_values = own_value.reshape(token_count, inner_width).astype(jnp.bfloat16)
    mixed = jnp.dot(attended_context, w_out, preferred_element_type=jnp.float32).astype(
        jnp.bfloat16
    )
    grad_in = (
        product("te,de->td", query_gradient_rows, w_query)
        + product("te,de->td", grad_keys, w_key)
        + product("te,de->td", grad_values, w_value)
    )
    weight_terms = (
        product("td,te->de", inputs, query_gradient_rows),
        product("td,te->de", inputs, grad_keys),
        product("td,te->de", inputs, grad_values),
        product("te,td->ed", attended_context, grad_out),
    )
    summed = lax.psum(
        (weight_terms[0], weight_terms[1], weight_terms[2], weight_terms[3]), ("dp", "seq")
    )
    return (
        mixed[None],
        grad_in.astype(jnp.bfloat16)[None],
        summed[0],
        summed[1],
        summed[2],
        summed[3],
    )


def solution(mesh):
    placed = (P("dp", "seq", None), P("dp", None), P(), P(), P(), P(), P("dp", "seq", None))
    return jax.shard_map(
        local,
        mesh=mesh,
        in_specs=placed,
        out_specs=(P("dp", "seq", None), P("dp", "seq", None), P(), P(), P(), P()),
        check_vma=False,
    )
```

profile of v0, /device:TPU:0, one launch (start us, length us, event | category | flops | bytes accessed | tf_op | source)
XLA Modules:
  0.0 892.1 jit_solution(2226027036387687723)
XLA Ops:
  11.3 6.8 collective-permute-start.7
  36.9 22.4 %all-gather = bf16[16,4,512]{2,1,0:T(4,128)(2,1)S(1)} all-gather(bf16[1,4,512]{2,1,0:T(4,128)(2,1)S(1)} %get-tuple-element.209), channel_id=1, replica_groups=mesh['dp'=2,'seq'=16] {'seq'}, dimensions={0}, use_global_device_ids=true | all-gather | bytes 69632 | tf_op jit(solution)/shard_map/all_gather | solution.py:152
  71.9 26.4 %collective-permute-start.1 = (bf16[2,512,512]{2,1,0:T(8,128)(2,1)}, bf16[2,512,512]{2,1,0:T(8,128)(2,1)}, u32[]{:S(2)}, u32[]{:S(2)}) collective-permute-start(bf16[2,512,512]{2,1,0:T(8,128)(2,1)} %pad_maximum_fusion.2), channel_id=1, source_target_pairs={{0,2},{1,3},{2,4},{3,5},{4,6},{5,7},{6,8},{7,9},{8,10},{9,11},{10,... | collective-permute-start | bytes 3145736 | tf_op jit(solution)/shard_map/ppermute | solution.py:17
  100.8 20.4 %collective-permute-start.6 = (bf16[4,512,512]{2,1,0:T(8,128)(2,1)}, bf16[4,512,512]{2,1,0:T(8,128)(2,1)}, u32[]{:S(2)}, u32[]{:S(2)}) collective-permute-start(bf16[4,512,512]{2,1,0:T(8,128)(2,1)} %pad_maximum_fusion.1), channel_id=1, source_target_pairs={{0,4},{1,5},{2,6},{3,7},{4,8},{5,9},{6,10},{7,11},{8,12},{9,13},{1... | collective-permute-start | bytes 6291464 | tf_op jit(solution)/shard_map/ppermute | solution.py:17
  128.3 63.2 %all-gather.1 = bf16[16,4,512]{2,1,0:T(4,128)(2,1)S(1)} all-gather(bf16[1,4,512]{2,1,0:T(4,128)(2,1)S(1)} %get-tuple-element.208), channel_id=1, replica_groups=mesh['dp'=2,'seq'=16] {'seq'}, dimensions={0}, use_global_device_ids=true | all-gather | bytes 69632 | tf_op jit(solution)/shard_map/all_gather | solution.py:153
  234.9 8.2 reshape.634
  275.9 7.7 reshape.631
  297.3 6.0 convolution_bitcast_fusion
  307.0 6.5 multiply_reduce_fusion
  313.6 9.6 %copy.235 = f32[4,1152,4,128]{3,1,2,0:T(8,128)} copy(f32[4,1152,4,128]{1,3,2,0:T(8,128)} %convolution_bitcast_fusion) | data formatting | bytes 18874368 | tf_op jit(solution)/shard_map/while/body/eval_jaxpr/ghqk,gqhe->gkhe/transpose | solution.py:21
  326.8 8.2 multiply_convert_fusion
  342.2 9.6 %copy.221 = f32[4,1152,4,128]{3,1,2,0:T(8,128)} copy(f32[4,1152,4,128]{1,3,2,0:T(8,128)} %convolution_bitcast_fusion.1) | data formatting | bytes 18874368 | tf_op jit(solution)/shard_map/while/body/eval_jaxpr/ghqk,gqhe->gkhe/transpose | solution.py:21
  397.3 15.6 %copy.230 = f32[36,128,4,128]{3,2,1,0:T(4,128)} copy(f32[36,128,4,128]{3,1,2,0:T(8,128)} %constant_dynamic-update-slice_fusion.18) | data formatting | bytes 18874368 | tf_op jit(solution)/shard_map/while/body/eval_jaxpr/dynamic_update_slice | solution.py:124
  415.3 16.0 %copy.244 = f32[36,128,4,128]{3,2,1,0:T(4,128)} copy(f32[36,128,4,128]{3,1,2,0:T(8,128)} %constant_dynamic-update-slice_fusion.17) | data formatting | bytes 18874368 | tf_op jit(solution)/shard_map/while/body/eval_jaxpr/dynamic_update_slice | solution.py:124
  431.3 12.3 %reshape.642 = f32[9,512,512]{2,1,0:T(8,128)} reshape(f32[36,128,4,128]{3,2,1,0:T(4,128)} %copy.230) | data formatting | bytes 18874368 | tf_op jit(solution)/shard_map/reshape | solution.py:227
  443.6 8.4 rev.14
  457.5 12.3 %reshape.647 = f32[9,512,512]{2,1,0:T(8,128)} reshape(f32[36,128,4,128]{3,2,1,0:T(4,128)} %copy.244) | data formatting | bytes 18874368 | tf_op jit(solution)/shard_map/reshape | solution.py:228
  469.7 8.4 rev.15
  495.5 7.2 fusion.11
  510.6 27.8 %collective-permute-done.9 = bf16[4,512,512]{2,1,0:T(8,128)(2,1)} collective-permute-done((bf16[4,512,512]{2,1,0:T(8,128)(2,1)}, bf16[4,512,512]{2,1,0:T(8,128)(2,1)}, u32[]{:S(2)}, u32[]{:S(2)}) %collective-permute-start.9) | collective-permute-done | bytes 2097184 | tf_op jit(solution)/shard_map/ppermute | solution.py:17
  544.9 38.5 %collective-permute-done.13 = bf16[4,512,512]{2,1,0:T(8,128)(2,1)} collective-permute-done((bf16[4,512,512]{2,1,0:T(8,128)(2,1)}, bf16[4,512,512]{2,1,0:T(8,128)(2,1)}, u32[]{:S(2)}, u32[]{:S(2)}) %collective-permute-start.13) | collective-permute-done | bytes 2097184 | tf_op jit(solution)/shard_map/ppermute | solution.py:17
  599.4 16.8 %collective-permute-done.14 = bf16[2,512,512]{2,1,0:T(8,128)(2,1)} collective-permute-done((bf16[2,512,512]{2,1,0:T(8,128)(2,1)}, bf16[2,512,512]{2,1,0:T(8,128)(2,1)}, u32[]{:S(2)}, u32[]{:S(2)}) %collective-permute-start.14) | collective-permute-done | bytes 1048608 | tf_op jit(solution)/shard_map/ppermute | solution.py:17
  623.6 63.3 %all-reduce.12.cloned.1.call-done = (bf16[64,4,128]{2,0,1:T(8,128)(2,1)}, bf16[64,4,128]{2,0,1:T(8,128)(2,1)}) async-done(((bf16[64,4,128]{2,0,1:T(8,128)(2,1)}, bf16[64,4,128]{2,0,1:T(8,128)(2,1)}), (bf16[64,4,128]{2,0,1:T(8,128)(2,1)}, bf16[64,4,128]{2,0,1:T(8,128)(2,1)})) %all-reduce.12.cloned.1.call-update) | async-done | bytes 131088
  703.6 171.3 %all-reduce.10.cloned.1.call-done = (f32[1024,512]{0,1:T(8,128)}, f32[1024,512]{0,1:T(8,128)}, f32[1024,512]{0,1:T(8,128)}, f32[512,1024]{1,0:T(8,128)}) async-done(((f32[1024,512]{0,1:T(8,128)}, f32[1024,512]{0,1:T(8,128)}, f32[1024,512]{0,1:T(8,128)}, f32[512,1024]{1,0:T(8,128)}), (f32[1024,512]{0,1:T(8,128)}, f32[1024,512]{0,1:T(8,128)}, f32[1024,512]{0,1:T(8,128)}, ...) | async-done | bytes 8388624 | tf_op jit(solution)/shard_map/psum | solution.py:286
  (309 shorter events, 283.2 us)
Async XLA Ops:
  7.2 679.7 %all-reduce.12.cloned.1.call-start = ((), (), s32[]{:S(2)}) async-start(), calls=%async_computation.1 | async-start | bytes 262144
  11.3 185.7 %collective-permute-start.7 = (bf16[1,512,512]{2,1,0:T(8,128)(2,1)}, bf16[1,512,512]{2,1,0:T(8,128)(2,1)}, u32[]{:S(2)}, u32[]{:S(2)}) collective-permute-start(bf16[1,512,512]{2,1,0:T(8,128)(2,1)} %bitcast.19), channel_id=1, source_target_pairs={{0,8},{1,9},{2,10},{3,11},{4,12},{5,13},{6,14},{7,15},{16,24},{17,... | collective-permute-start | bytes 1572872 | tf_op jit(solution)/shard_map/ppermute | solution.py:17
  18.1 43.3 %collective-permute-start.4 = (bf16[1,512,512]{2,1,0:T(8,128)(2,1)}, bf16[1,512,512]{2,1,0:T(8,128)(2,1)S(1)}, u32[]{:S(2)}, u32[]{:S(2)}) collective-permute-start(bf16[1,512,512]{2,1,0:T(8,128)(2,1)} %bitcast.19), channel_id=1, source_target_pairs={{0,1},{1,2},{2,3},{3,4},{4,5},{5,6},{6,7},{7,8},{8,9},{9,10},{10,1... | collective-permute-start | bytes 1572872 | tf_op jit(solution)/shard_map/ppermute | solution.py:17
  22.3 176.6 %collective-permute-start.3 = (bf16[1,512,512]{2,1,0:T(8,128)(2,1)S(1)}, bf16[1,512,512]{2,1,0:T(8,128)(2,1)}, u32[]{:S(2)}, u32[]{:S(2)}) collective-permute-start(bf16[1,512,512]{2,1,0:T(8,128)(2,1)S(1)} %bitcast.382), channel_id=1, source_target_pairs={{0,8},{1,9},{2,10},{3,11},{4,12},{5,13},{6,14},{7,15},{16,24},{17,... | collective-permute-start | bytes 1572872 | tf_op jit(solution)/shard_map/ppermute | solution.py:17
  24.4 45.4 %collective-permute-start = (bf16[1,512,512]{2,1,0:T(8,128)(2,1)S(1)}, bf16[1,512,512]{2,1,0:T(8,128)(2,1)}, u32[]{:S(2)}, u32[]{:S(2)}) collective-permute-start(bf16[1,512,512]{2,1,0:T(8,128)(2,1)S(1)} %bitcast.383), channel_id=1, source_target_pairs={{0,1},{1,2},{2,3},{3,4},{4,5},{5,6},{6,7},{7,8},{8,9},{9,10},{10,1... | collective-permute-start | bytes 1572872 | tf_op jit(solution)/shard_map/ppermute | solution.py:17
  62.7 35.5 %collective-permute-start.5 = (bf16[2,512,512]{2,1,0:T(8,128)(2,1)S(1)}, bf16[2,512,512]{2,1,0:T(8,128)(2,1)S(1)}, u32[]{:S(2)}, u32[]{:S(2)}) collective-permute-start(bf16[2,512,512]{2,1,0:T(8,128)(2,1)S(1)} %pad_maximum_fusion.3), channel_id=1, source_target_pairs={{0,2},{1,3},{2,4},{3,5},{4,6},{5,7},{6,8},{7,9},{8,10},{9,11},{10,... | collective-permute-start | bytes 3145736 | tf_op jit(solution)/shard_map/ppermute | solution.py:17
  71.9 119.7 %copy-start.50 = (u32[32]{0:T(128)S(1)}, u32[32]{0:T(128)}, u32[]{:S(2)}) copy-start(u32[32]{0:T(128)} %constant.355) | copy-start | bytes 388
  71.9 132.8 %collective-permute-start.1 = (bf16[2,512,512]{2,1,0:T(8,128)(2,1)}, bf16[2,512,512]{2,1,0:T(8,128)(2,1)}, u32[]{:S(2)}, u32[]{:S(2)}) collective-permute-start(bf16[2,512,512]{2,1,0:T(8,128)(2,1)} %pad_maximum_fusion.2), channel_id=1, source_target_pairs={{0,2},{1,3},{2,4},{3,5},{4,6},{5,7},{6,8},{7,9},{8,10},{9,11},{10,... | collective-permute-start | bytes 3145736 | tf_op jit(solution)/shard_map/ppermute | solution.py:17
  100.8 124.3 %collective-permute-start.6 = (bf16[4,512,512]{2,1,0:T(8,128)(2,1)}, bf16[4,512,512]{2,1,0:T(8,128)(2,1)}, u32[]{:S(2)}, u32[]{:S(2)}) collective-permute-start(bf16[4,512,512]{2,1,0:T(8,128)(2,1)} %pad_maximum_fusion.1), channel_id=1, source_target_pairs={{0,4},{1,5},{2,6},{3,7},{4,8},{5,9},{6,10},{7,11},{8,12},{9,13},{1... | collective-permute-start | bytes 6291464 | tf_op jit(solution)/shard_map/ppermute | solution.py:17
  127.2 64.9 %copy-start.22 = (bf16[4,128,4,128]{3,2,1,0:T(4,128)(2,1)}, bf16[4,128,4,128]{3,2,1,0:T(4,128)(2,1)S(1)}, u32[]{:S(2)}) copy-start(bf16[4,128,4,128]{3,2,1,0:T(4,128)(2,1)S(1)} %reshape.639) | copy-start | bytes 1572868
  207.6 58.5 %collective-permute-start.2 = (bf16[4,512,512]{2,1,0:T(8,128)(2,1)}, bf16[4,512,512]{2,1,0:T(8,128)(2,1)}, u32[]{:S(2)}, u32[]{:S(2)}) collective-permute-start(bf16[4,512,512]{2,1,0:T(8,128)(2,1)} %pad_maximum_fusion), channel_id=1, source_target_pairs={{0,4},{1,5},{2,6},{3,7},{4,8},{5,9},{6,10},{7,11},{8,12},{9,13},{1... | collective-permute-start | bytes 6291464 | tf_op jit(solution)/shard_map/ppermute | solution.py:17
  372.1 109.3 %collective-permute-start.8 = (bf16[1,512,512]{2,1,0:T(8,128)(2,1)}, bf16[1,512,512]{2,1,0:T(8,128)(2,1)}, u32[]{:S(2)}, u32[]{:S(2)}) collective-permute-start(bf16[1,512,512]{2,1,0:T(8,128)(2,1)} %convert_element_type.176), channel_id=1, source_target_pairs={{8,0},{9,1},{10,2},{11,3},{12,4},{13,5},{14,6},{15,7},{24,16},{25,... | collective-permute-start | bytes 1572872 | tf_op jit(solution)/shard_map/ppermute | solution.py:17
  392.4 96.8 %collective-permute-start.12 = (bf16[1,512,512]{2,1,0:T(8,128)(2,1)}, bf16[1,512,512]{2,1,0:T(8,128)(2,1)S(1)}, u32[]{:S(2)}, u32[]{:S(2)}) collective-permute-start(bf16[1,512,512]{2,1,0:T(8,128)(2,1)} %convert_element_type.185), channel_id=1, source_target_pairs={{8,0},{9,1},{10,2},{11,3},{12,4},{13,5},{14,6},{15,7},{24,16},{25,... | collective-permute-start | bytes 1572872 | tf_op jit(solution)/shard_map/ppermute | solution.py:17
  487.7 50.7 %collective-permute-start.9 = (bf16[4,512,512]{2,1,0:T(8,128)(2,1)}, bf16[4,512,512]{2,1,0:T(8,128)(2,1)}, u32[]{:S(2)}, u32[]{:S(2)}) collective-permute-start(bf16[4,512,512]{2,1,0:T(8,128)(2,1)} %slice.541), channel_id=1, source_target_pairs={{4,0},{5,1},{6,2},{7,3},{8,4},{9,5},{10,6},{11,7},{12,8},{13,9},{1... | collective-permute-start | bytes 6291464 | tf_op jit(solution)/shard_map/ppermute | solution.py:17
  494.1 89.2 %collective-permute-start.13 = (bf16[4,512,512]{2,1,0:T(8,128)(2,1)}, bf16[4,512,512]{2,1,0:T(8,128)(2,1)}, u32[]{:S(2)}, u32[]{:S(2)}) collective-permute-start(bf16[4,512,512]{2,1,0:T(8,128)(2,1)} %slice.540), channel_id=1, source_target_pairs={{4,0},{5,1},{6,2},{7,3},{8,4},{9,5},{10,6},{11,7},{12,8},{13,9},{1... | collective-permute-start | bytes 6291464 | tf_op jit(solution)/shard_map/ppermute | solution.py:17
  503.7 88.7 %copy-start.20 = (bf16[4,128,4,128]{3,2,1,0:T(4,128)(2,1)}, bf16[4,128,4,128]{3,2,1,0:T(4,128)(2,1)S(1)}, u32[]{:S(2)}) copy-start(bf16[4,128,4,128]{3,2,1,0:T(4,128)(2,1)S(1)} %copy.210) | copy-start | bytes 1572868
  543.3 49.1 %copy-start.36 = (bf16[1,512,1024]{2,1,0:T(8,128)(2,1)S(1)}, bf16[1,512,1024]{2,1,0:T(8,128)(2,1)}, u32[]{:S(2)}) copy-start(bf16[1,512,1024]{2,1,0:T(8,128)(2,1)} %param.29) | copy-start | bytes 3145732
  543.3 51.2 %collective-permute-start.10 = (bf16[2,512,512]{2,1,0:T(8,128)(2,1)}, bf16[2,512,512]{2,1,0:T(8,128)(2,1)}, u32[]{:S(2)}, u32[]{:S(2)}) collective-permute-start(bf16[2,512,512]{2,1,0:T(8,128)(2,1)} %slice.543), channel_id=1, source_target_pairs={{2,0},{3,1},{4,2},{5,3},{6,4},{7,5},{8,6},{9,7},{10,8},{11,9},{12,... | collective-permute-start | bytes 3145736 | tf_op jit(solution)/shard_map/ppermute | solution.py:17
  589.3 26.9 %collective-permute-start.14 = (bf16[2,512,512]{2,1,0:T(8,128)(2,1)}, bf16[2,512,512]{2,1,0:T(8,128)(2,1)}, u32[]{:S(2)}, u32[]{:S(2)}) collective-permute-start(bf16[2,512,512]{2,1,0:T(8,128)(2,1)} %slice.542), channel_id=1, source_target_pairs={{2,0},{3,1},{4,2},{5,3},{6,4},{7,5},{8,6},{9,7},{10,8},{11,9},{12,... | collective-permute-start | bytes 3145736 | tf_op jit(solution)/shard_map/ppermute | solution.py:17
  592.3 282.6 %all-reduce.10.cloned.1.call-start = ((), (), s32[]{:S(2)}) async-start(), calls=%async_computation | async-start | bytes 16777216 | tf_op jit(solution)/shard_map/psum | solution.py:286
  598.0 88.9 %copy-start.49 = (f32[4]{0:T(128)S(1)}, f32[4]{0:T(128)}, u32[]{:S(2)}) copy-start(f32[4]{0:T(128)} %get-tuple-element.184) | copy-start | bytes 52
  598.0 89.7 %collective-permute-start.11 = (bf16[1,512,512]{2,1,0:T(8,128)(2,1)}, bf16[1,512,512]{2,1,0:T(8,128)(2,1)}, u32[]{:S(2)}, u32[]{:S(2)}) collective-permute-start(bf16[1,512,512]{2,1,0:T(8,128)(2,1)} %slice.545), channel_id=1, source_target_pairs={{1,0},{2,1},{3,2},{4,3},{5,4},{6,5},{7,6},{8,7},{9,8},{10,9},{11,1... | collective-permute-start | bytes 1572872 | tf_op jit(solution)/shard_map/ppermute | solution.py:17
  619.1 68.8 %copy-start.46 = (pred[512]{0:T(512)(128)(4,1)S(1)}, pred[512]{0:T(512)(128)(4,1)}, u32[]{:S(2)}) copy-start(pred[512]{0:T(512)(128)(4,1)} %copy-done.45) | copy-start | bytes 1540
  620.0 67.7 %collective-permute-start.15 = (bf16[1,512,512]{2,1,0:T(8,128)(2,1)}, bf16[1,512,512]{2,1,0:T(8,128)(2,1)}, u32[]{:S(2)}, u32[]{:S(2)}) collective-permute-start(bf16[1,512,512]{2,1,0:T(8,128)(2,1)} %slice.544), channel_id=1, source_target_pairs={{1,0},{2,1},{3,2},{4,3},{5,4},{6,5},{7,6},{8,7},{9,8},{10,9},{11,1... | collective-permute-start | bytes 1572872 | tf_op jit(solution)/shard_map/ppermute | solution.py:17
  (47 other events, 565.7 us)
Sparse Core Ops, SparseCore 0:
  592.5 94.3 all-reduce.11
  694.2 180.7 all-reduce.9
where the time goes:
time: 903 us; the launch traced here: 892 us
  waiting for transfers between devices  318 us (35%)
  local copies, waits for them, and re-layouts  256 us (28%)
  blocking collectives  85.6 us (9%)
  starting transfers between devices  81 us (9%)
  matrix products  68.2 us (8%)
  other arithmetic  67.7 us (7%)
  between operations  16 us (2%)
    psum x1, waiting for transfers between devices, local(): lax.psum((weight_terms[0], weight_terms[1], weight_terms[2], weight_terms...  171 us
    ppermute x16, waiting for transfers between devices, shifted(): return lax.ppermute(block, axis, route)  83.1 us
    ppermute x16, starting transfers between devices, shifted(): return lax.ppermute(block, axis, route)  81 us
    unnamed x3, waiting for transfers between devices  63.4 us
    all_gather x1, blocking collectives, local(): lax.all_gather(own_summary[1], 'seq', axis=0, tiled=True)  63.2 us
    dot_general x19, matrix products, product(): return jnp.einsum(form, left, right, preferred_element_type=jnp.float32)  53.6 us
    unnamed x134, local copies, waits for them, and re-layouts  53.4 us
    dynamic_update_slice x6, local copies, waits for them, and re-layouts, spread(): lax.dynamic_update_slice_in_dim(running, current + grads[:, position], fi...  36.1 us
  transfers between devices with their start and end apart: 18, of which 5 were waited for; matrix products, arithmetic and copies ran while one was open for 29% of the time, Pallas kernels for 0%

commit v1 on v0

--- a/solution.py
+++ b/solution.py
@@ -284,7 +284,7 @@
         product("te,td->ed", attended_context, grad_out),
     )
     summed = lax.psum(
-        (weight_terms[0], weight_terms[1], weight_terms[2], weight_terms[3]), ("dp", "seq")
+        lax.psum((weight_terms[0], weight_terms[1], weight_terms[2], weight_terms[3]), "seq"), "dp"
     )
     return (
         mixed[None],

time: 903 us -> 1090 us (1.21)
  waiting for transfers between devices: 318 us -> 509 us
    psum x0 -> x1, waiting for transfers between devices: none -> 191 us  [local(): lax.psum(lax.psum((weight_terms[0], weight_terms[1], weight_terms[2], wei...]
    unnamed x3 -> x4, waiting for transfers between devices: 63.4 us -> 63.6 us
  transfers between devices with their start and end apart: 18 -> 19, of which waited for: 5 -> 6; matrix products, arithmetic and copies ran while one was open for 29% -> 24% of each run, Pallas kernels for 0% -> 0%
where the time goes in v1:
time: 1090 us; the launch traced here: 1080 us
  waiting for transfers between devices  509 us (47%)
  local copies, waits for them, and re-layouts  255 us (23%)
  blocking collectives  85.7 us (8%)
  starting transfers between devices  81.2 us (7%)
  matrix products  68.6 us (6%)
  other arithmetic  67.6 us (6%)
  between operations  15.7 us (1%)
    psum x1, waiting for transfers between devices, local(): lax.psum(lax.psum((weight_terms[0], weight_terms[1], weight_terms[2], wei...  191 us
    psum x1, waiting for transfers between devices, local(): lax.psum((weight_terms[0], weight_terms[1], weight_terms[2], weight_terms...  172 us
    ppermute x16, waiting for transfers between devices, shifted(): return lax.ppermute(block, axis, route)  82.9 us
    ppermute x16, starting transfers between devices, shifted(): return lax.ppermute(block, axis, route)  80.9 us
    unnamed x4, waiting for transfers between devices  63.6 us
    all_gather x1, blocking collectives, local(): lax.all_gather(own_summary[1], 'seq', axis=0, tiled=True)  63.2 us
    dot_general x19, matrix products, product(): return jnp.einsum(form, left, right, preferred_element_type=jnp.float32)  53.9 us
    unnamed x134, local copies, waits for them, and re-layouts  53.4 us
  transfers between devices with their start and end apart: 19, of which 6 were waited for; matrix products, arithmetic and copies ran while one was open for 24% of the time, Pallas kernels for 0%

profile of v1, /device:TPU:0, one launch (start us, length us, event | category | flops | bytes accessed | tf_op | source)
XLA Modules:
  0.0 1083.4 jit_solution(14594865241269398414)
XLA Ops:
  11.3 6.8 collective-permute-start.7
  36.8 22.5 %all-gather = bf16[16,4,512]{2,1,0:T(4,128)(2,1)S(1)} all-gather(bf16[1,4,512]{2,1,0:T(4,128)(2,1)S(1)} %get-tuple-element.213), channel_id=1, replica_groups=mesh['dp'=2,'seq'=16] {'seq'}, dimensions={0}, use_global_device_ids=true | all-gather | bytes 69632 | tf_op jit(solution)/shard_map/all_gather | solution.py:152
  71.9 26.4 %collective-permute-start.1 = (bf16[2,512,512]{2,1,0:T(8,128)(2,1)}, bf16[2,512,512]{2,1,0:T(8,128)(2,1)}, u32[]{:S(2)}, u32[]{:S(2)}) collective-permute-start(bf16[2,512,512]{2,1,0:T(8,128)(2,1)} %pad_maximum_fusion.2), channel_id=1, source_target_pairs={{0,2},{1,3},{2,4},{3,5},{4,6},{5,7},{6,8},{7,9},{8,10},{9,11},{10,... | collective-permute-start | bytes 3145736 | tf_op jit(solution)/shard_map/ppermute | solution.py:17
  100.8 20.4 %collective-permute-start.6 = (bf16[4,512,512]{2,1,0:T(8,128)(2,1)}, bf16[4,512,512]{2,1,0:T(8,128)(2,1)}, u32[]{:S(2)}, u32[]{:S(2)}) collective-permute-start(bf16[4,512,512]{2,1,0:T(8,128)(2,1)} %pad_maximum_fusion.1), channel_id=1, source_target_pairs={{0,4},{1,5},{2,6},{3,7},{4,8},{5,9},{6,10},{7,11},{8,12},{9,13},{1... | collective-permute-start | bytes 6291464 | tf_op jit(solution)/shard_map/ppermute | solution.py:17
  128.3 63.2 %all-gather.1 = bf16[16,4,512]{2,1,0:T(4,128)(2,1)S(1)} all-gather(bf16[1,4,512]{2,1,0:T(4,128)(2,1)S(1)} %get-tuple-element.212), channel_id=1, replica_groups=mesh['dp'=2,'seq'=16] {'seq'}, dimensions={0}, use_global_device_ids=true | all-gather | bytes 69632 | tf_op jit(solution)/shard_map/all_gather | solution.py:153
  234.9 8.0 reshape.634
  275.8 7.7 reshape.631
  306.9 6.9 multiply_reduce_fusion
  313.8 9.6 copy.235
  327.0 8.2 multiply_convert_fusion
  342.4 9.6 copy.221
  397.5 15.6 %copy.230 = f32[36,128,4,128]{3,2,1,0:T(4,128)} copy(f32[36,128,4,128]{3,1,2,0:T(8,128)} %constant_dynamic-update-slice_fusion.18) | data formatting | bytes 18874368 | tf_op jit(solution)/shard_map/while/body/eval_jaxpr/dynamic_update_slice | solution.py:124
  415.5 15.8 %copy.244 = f32[36,128,4,128]{3,2,1,0:T(4,128)} copy(f32[36,128,4,128]{3,1,2,0:T(8,128)} %constant_dynamic-update-slice_fusion.17) | data formatting | bytes 18874368 | tf_op jit(solution)/shard_map/while/body/eval_jaxpr/dynamic_update_slice | solution.py:124
  431.3 12.3 %reshape.642 = f32[9,512,512]{2,1,0:T(8,128)} reshape(f32[36,128,4,128]{3,2,1,0:T(4,128)} %copy.230) | data formatting | bytes 18874368 | tf_op jit(solution)/shard_map/reshape | solution.py:227
  443.6 8.4 rev.14
  457.5 12.3 %reshape.647 = f32[9,512,512]{2,1,0:T(8,128)} reshape(f32[36,128,4,128]{3,2,1,0:T(4,128)} %copy.244) | data formatting | bytes 18874368 | tf_op jit(solution)/shard_map/reshape | solution.py:228
  469.7 8.4 rev.15
  495.8 7.2 fusion.11
  510.8 27.6 %collective-permute-done.9 = bf16[4,512,512]{2,1,0:T(8,128)(2,1)} collective-permute-done((bf16[4,512,512]{2,1,0:T(8,128)(2,1)}, bf16[4,512,512]{2,1,0:T(8,128)(2,1)}, u32[]{:S(2)}, u32[]{:S(2)}) %collective-permute-start.9) | collective-permute-done | bytes 2097184 | tf_op jit(solution)/shard_map/ppermute | solution.py:17
  544.8 38.5 %collective-permute-done.13 = bf16[4,512,512]{2,1,0:T(8,128)(2,1)} collective-permute-done((bf16[4,512,512]{2,1,0:T(8,128)(2,1)}, bf16[4,512,512]{2,1,0:T(8,128)(2,1)}, u32[]{:S(2)}, u32[]{:S(2)}) %collective-permute-start.13) | collective-permute-done | bytes 2097184 | tf_op jit(solution)/shard_map/ppermute | solution.py:17
  599.4 16.8 %collective-permute-done.14 = bf16[2,512,512]{2,1,0:T(8,128)(2,1)} collective-permute-done((bf16[2,512,512]{2,1,0:T(8,128)(2,1)}, bf16[2,512,512]{2,1,0:T(8,128)(2,1)}, u32[]{:S(2)}, u32[]{:S(2)}) %collective-permute-start.14) | collective-permute-done | bytes 1048608 | tf_op jit(solution)/shard_map/ppermute | solution.py:17
  623.4 63.6 %all-reduce.16.cloned.1.call-done = (bf16[64,4,128]{2,0,1:T(8,128)(2,1)}, bf16[64,4,128]{2,0,1:T(8,128)(2,1)}) async-done(((bf16[64,4,128]{2,0,1:T(8,128)(2,1)}, bf16[64,4,128]{2,0,1:T(8,128)(2,1)}), (bf16[64,4,128]{2,0,1:T(8,128)(2,1)}, bf16[64,4,128]{2,0,1:T(8,128)(2,1)})) %all-reduce.16.cloned.1.call-update) | async-done | bytes 131088
  694.3 171.7 %all-reduce.12.cloned.1.call-done = (f32[1024,512]{0,1:T(8,128)}, f32[1024,512]{0,1:T(8,128)}, f32[1024,512]{0,1:T(8,128)}, f32[512,1024]{1,0:T(8,128)}) async-done(((f32[1024,512]{0,1:T(8,128)}, f32[1024,512]{0,1:T(8,128)}, f32[1024,512]{0,1:T(8,128)}, f32[512,1024]{1,0:T(8,128)}), (f32[1024,512]{0,1:T(8,128)}, f32[1024,512]{0,1:T(8,128)}, f32[1024,512]{0,1:T(8,128)}, ...) | async-done | bytes 8388624 | tf_op jit(solution)/shard_map/psum | solution.py:287
  875.6 191.0 %all-reduce.14.cloned.1.call-done = (f32[1024,512]{0,1:T(8,128)}, f32[1024,512]{0,1:T(8,128)}, f32[1024,512]{0,1:T(8,128)}, f32[512,1024]{1,0:T(8,128)}) async-done(((f32[1024,512]{0,1:T(8,128)}, f32[1024,512]{0,1:T(8,128)}, f32[1024,512]{0,1:T(8,128)}, f32[512,1024]{1,0:T(8,128)}), (f32[1024,512]{0,1:T(8,128)}, f32[1024,512]{0,1:T(8,128)}, f32[1024,512]{0,1:T(8,128)}, ...) | async-done | bytes 8388624 | tf_op jit(solution)/shard_map/psum | solution.py:286
  (312 shorter events, 289.4 us)
Async XLA Ops:
  7.2 679.7 %all-reduce.16.cloned.1.call-start = ((), (), s32[]{:S(2)}) async-start(), calls=%async_computation.2 | async-start | bytes 262144
  11.3 185.7 %collective-permute-start.7 = (bf16[1,512,512]{2,1,0:T(8,128)(2,1)}, bf16[1,512,512]{2,1,0:T(8,128)(2,1)}, u32[]{:S(2)}, u32[]{:S(2)}) collective-permute-start(bf16[1,512,512]{2,1,0:T(8,128)(2,1)} %bitcast.19), channel_id=1, source_target_pairs={{0,8},{1,9},{2,10},{3,11},{4,12},{5,13},{6,14},{7,15},{16,24},{17,... | collective-permute-start | bytes 1572872 | tf_op jit(solution)/shard_map/ppermute | solution.py:17
  18.1 43.3 %collective-permute-start.4 = (bf16[1,512,512]{2,1,0:T(8,128)(2,1)}, bf16[1,512,512]{2,1,0:T(8,128)(2,1)S(1)}, u32[]{:S(2)}, u32[]{:S(2)}) collective-permute-start(bf16[1,512,512]{2,1,0:T(8,128)(2,1)} %bitcast.19), channel_id=1, source_target_pairs={{0,1},{1,2},{2,3},{3,4},{4,5},{5,6},{6,7},{7,8},{8,9},{9,10},{10,1... | collective-permute-start | bytes 1572872 | tf_op jit(solution)/shard_map/ppermute | solution.py:17
  22.3 176.6 %collective-permute-start.3 = (bf16[1,512,512]{2,1,0:T(8,128)(2,1)S(1)}, bf16[1,512,512]{2,1,0:T(8,128)(2,1)}, u32[]{:S(2)}, u32[]{:S(2)}) collective-permute-start(bf16[1,512,512]{2,1,0:T(8,128)(2,1)S(1)} %bitcast.382), channel_id=1, source_target_pairs={{0,8},{1,9},{2,10},{3,11},{4,12},{5,13},{6,14},{7,15},{16,24},{17,... | collective-permute-start | bytes 1572872 | tf_op jit(solution)/shard_map/ppermute | solution.py:17
  24.4 45.4 %collective-permute-start = (bf16[1,512,512]{2,1,0:T(8,128)(2,1)S(1)}, bf16[1,512,512]{2,1,0:T(8,128)(2,1)}, u32[]{:S(2)}, u32[]{:S(2)}) collective-permute-start(bf16[1,512,512]{2,1,0:T(8,128)(2,1)S(1)} %bitcast.383), channel_id=1, source_target_pairs={{0,1},{1,2},{2,3},{3,4},{4,5},{5,6},{6,7},{7,8},{8,9},{9,10},{10,1... | collective-permute-start | bytes 1572872 | tf_op jit(solution)/shard_map/ppermute | solution.py:17
  62.7 35.5 %collective-permute-start.5 = (bf16[2,512,512]{2,1,0:T(8,128)(2,1)S(1)}, bf16[2,512,512]{2,1,0:T(8,128)(2,1)S(1)}, u32[]{:S(2)}, u32[]{:S(2)}) collective-permute-start(bf16[2,512,512]{2,1,0:T(8,128)(2,1)S(1)} %pad_maximum_fusion.3), channel_id=1, source_target_pairs={{0,2},{1,3},{2,4},{3,5},{4,6},{5,7},{6,8},{7,9},{8,10},{9,11},{10,... | collective-permute-start | bytes 3145736 | tf_op jit(solution)/shard_map/ppermute | solution.py:17
  71.9 119.7 %copy-start.50 = (u32[32]{0:T(128)S(1)}, u32[32]{0:T(128)}, u32[]{:S(2)}) copy-start(u32[32]{0:T(128)} %constant.355) | copy-start | bytes 388
  71.9 132.9 %collective-permute-start.1 = (bf16[2,512,512]{2,1,0:T(8,128)(2,1)}, bf16[2,512,512]{2,1,0:T(8,128)(2,1)}, u32[]{:S(2)}, u32[]{:S(2)}) collective-permute-start(bf16[2,512,512]{2,1,0:T(8,128)(2,1)} %pad_maximum_fusion.2), channel_id=1, source_target_pairs={{0,2},{1,3},{2,4},{3,5},{4,6},{5,7},{6,8},{7,9},{8,10},{9,11},{10,... | collective-permute-start | bytes 3145736 | tf_op jit(solution)/shard_map/ppermute | solution.py:17
  100.8 124.4 %collective-permute-start.6 = (bf16[4,512,512]{2,1,0:T(8,128)(2,1)}, bf16[4,512,512]{2,1,0:T(8,128)(2,1)}, u32[]{:S(2)}, u32[]{:S(2)}) collective-permute-start(bf16[4,512,512]{2,1,0:T(8,128)(2,1)} %pad_maximum_fusion.1), channel_id=1, source_target_pairs={{0,4},{1,5},{2,6},{3,7},{4,8},{5,9},{6,10},{7,11},{8,12},{9,13},{1... | collective-permute-start | bytes 6291464 | tf_op jit(solution)/shard_map/ppermute | solution.py:17
  127.2 64.9 %copy-start.22 = (bf16[4,128,4,128]{3,2,1,0:T(4,128)(2,1)}, bf16[4,128,4,128]{3,2,1,0:T(4,128)(2,1)S(1)}, u32[]{:S(2)}) copy-start(bf16[4,128,4,128]{3,2,1,0:T(4,128)(2,1)S(1)} %reshape.639) | copy-start | bytes 1572868
  207.6 58.4 %collective-permute-start.2 = (bf16[4,512,512]{2,1,0:T(8,128)(2,1)}, bf16[4,512,512]{2,1,0:T(8,128)(2,1)}, u32[]{:S(2)}, u32[]{:S(2)}) collective-permute-start(bf16[4,512,512]{2,1,0:T(8,128)(2,1)} %pad_maximum_fusion), channel_id=1, source_target_pairs={{0,4},{1,5},{2,6},{3,7},{4,8},{5,9},{6,10},{7,11},{8,12},{9,13},{1... | collective-permute-start | bytes 6291464 | tf_op jit(solution)/shard_map/ppermute | solution.py:17
  372.3 109.1 %collective-permute-start.8 = (bf16[1,512,512]{2,1,0:T(8,128)(2,1)}, bf16[1,512,512]{2,1,0:T(8,128)(2,1)}, u32[]{:S(2)}, u32[]{:S(2)}) collective-permute-start(bf16[1,512,512]{2,1,0:T(8,128)(2,1)} %convert_element_type.176), channel_id=1, source_target_pairs={{8,0},{9,1},{10,2},{11,3},{12,4},{13,5},{14,6},{15,7},{24,16},{25,... | collective-permute-start | bytes 1572872 | tf_op jit(solution)/shard_map/ppermute | solution.py:17
  392.6 96.8 %collective-permute-start.12 = (bf16[1,512,512]{2,1,0:T(8,128)(2,1)}, bf16[1,512,512]{2,1,0:T(8,128)(2,1)S(1)}, u32[]{:S(2)}, u32[]{:S(2)}) collective-permute-start(bf16[1,512,512]{2,1,0:T(8,128)(2,1)} %convert_element_type.185), channel_id=1, source_target_pairs={{8,0},{9,1},{10,2},{11,3},{12,4},{13,5},{14,6},{15,7},{24,16},{25,... | collective-permute-start | bytes 1572872 | tf_op jit(solution)/shard_map/ppermute | solution.py:17
  487.7 50.7 %collective-permute-start.9 = (bf16[4,512,512]{2,1,0:T(8,128)(2,1)}, bf16[4,512,512]{2,1,0:T(8,128)(2,1)}, u32[]{:S(2)}, u32[]{:S(2)}) collective-permute-start(bf16[4,512,512]{2,1,0:T(8,128)(2,1)} %slice.541), channel_id=1, source_target_pairs={{4,0},{5,1},{6,2},{7,3},{8,4},{9,5},{10,6},{11,7},{12,8},{13,9},{1... | collective-permute-start | bytes 6291464 | tf_op jit(solution)/shard_map/ppermute | solution.py:17
  494.3 89.0 %collective-permute-start.13 = (bf16[4,512,512]{2,1,0:T(8,128)(2,1)}, bf16[4,512,512]{2,1,0:T(8,128)(2,1)}, u32[]{:S(2)}, u32[]{:S(2)}) collective-permute-start(bf16[4,512,512]{2,1,0:T(8,128)(2,1)} %slice.540), channel_id=1, source_target_pairs={{4,0},{5,1},{6,2},{7,3},{8,4},{9,5},{10,6},{11,7},{12,8},{13,9},{1... | collective-permute-start | bytes 6291464 | tf_op jit(solution)/shard_map/ppermute | solution.py:17
  503.9 88.4 %copy-start.20 = (bf16[4,128,4,128]{3,2,1,0:T(4,128)(2,1)}, bf16[4,128,4,128]{3,2,1,0:T(4,128)(2,1)S(1)}, u32[]{:S(2)}) copy-start(bf16[4,128,4,128]{3,2,1,0:T(4,128)(2,1)S(1)} %copy.210) | copy-start | bytes 1572868
  543.3 51.2 %collective-permute-start.10 = (bf16[2,512,512]{2,1,0:T(8,128)(2,1)}, bf16[2,512,512]{2,1,0:T(8,128)(2,1)}, u32[]{:S(2)}, u32[]{:S(2)}) collective-permute-start(bf16[2,512,512]{2,1,0:T(8,128)(2,1)} %slice.543), channel_id=1, source_target_pairs={{2,0},{3,1},{4,2},{5,3},{6,4},{7,5},{8,6},{9,7},{10,8},{11,9},{12,... | collective-permute-start | bytes 3145736 | tf_op jit(solution)/shard_map/ppermute | solution.py:17
  589.3 26.9 %collective-permute-start.14 = (bf16[2,512,512]{2,1,0:T(8,128)(2,1)}, bf16[2,512,512]{2,1,0:T(8,128)(2,1)}, u32[]{:S(2)}, u32[]{:S(2)}) collective-permute-start(bf16[2,512,512]{2,1,0:T(8,128)(2,1)} %slice.542), channel_id=1, source_target_pairs={{2,0},{3,1},{4,2},{5,3},{6,4},{7,5},{8,6},{9,7},{10,8},{11,9},{12,... | collective-permute-start | bytes 3145736 | tf_op jit(solution)/shard_map/ppermute | solution.py:17
  592.3 273.7 %all-reduce.12.cloned.1.call-start = ((), (), s32[]{:S(2)}) async-start(), calls=%async_computation | async-start | bytes 16777216 | tf_op jit(solution)/shard_map/psum | solution.py:287
  598.0 88.9 %copy-start.49 = (f32[4]{0:T(128)S(1)}, f32[4]{0:T(128)}, u32[]{:S(2)}) copy-start(f32[4]{0:T(128)} %get-tuple-element.188) | copy-start | bytes 52
  598.0 89.7 %collective-permute-start.11 = (bf16[1,512,512]{2,1,0:T(8,128)(2,1)}, bf16[1,512,512]{2,1,0:T(8,128)(2,1)}, u32[]{:S(2)}, u32[]{:S(2)}) collective-permute-start(bf16[1,512,512]{2,1,0:T(8,128)(2,1)} %slice.545), channel_id=1, source_target_pairs={{1,0},{2,1},{3,2},{4,3},{5,4},{6,5},{7,6},{8,7},{9,8},{10,9},{11,1... | collective-permute-start | bytes 1572872 | tf_op jit(solution)/shard_map/ppermute | solution.py:17
  619.1 68.8 %copy-start.46 = (pred[512]{0:T(512)(128)(4,1)S(1)}, pred[512]{0:T(512)(128)(4,1)}, u32[]{:S(2)}) copy-start(pred[512]{0:T(512)(128)(4,1)} %copy-done.45) | copy-start | bytes 1540
  620.0 67.7 %collective-permute-start.15 = (bf16[1,512,512]{2,1,0:T(8,128)(2,1)}, bf16[1,512,512]{2,1,0:T(8,128)(2,1)}, u32[]{:S(2)}, u32[]{:S(2)}) collective-permute-start(bf16[1,512,512]{2,1,0:T(8,128)(2,1)} %slice.544), channel_id=1, source_target_pairs={{1,0},{2,1},{3,2},{4,3},{5,4},{6,5},{7,6},{8,7},{9,8},{10,9},{11,1... | collective-permute-start | bytes 1572872 | tf_op jit(solution)/shard_map/ppermute | solution.py:17
  694.1 372.5 %all-reduce.14.cloned.1.call-start = ((), (), s32[]{:S(2)}) async-start(), calls=%async_computation.1 | async-start | bytes 16777216 | tf_op jit(solution)/shard_map/psum | solution.py:286
  (48 other events, 614.9 us)
Sparse Core Ops, SparseCore 0:
  592.4 94.4 all-reduce.15
  694.2 171.7 all-reduce.11
  868.7 197.9 all-reduce.13
